TPU v7x, 32 devices: a whole 2x2x4 slice. The times are simulated.
32 devices in a mesh: row: 8 (over y, x, core), col: 4 (over z).
Axes of the slice: x: 2, y: 2, z: 4, core: 2. Of those that a mesh axis runs over, the one named last changes fastest.
Arguments:
- pair_factors: float32 [12288, 1024], P(('row', 'col')), may hold values from -0.09375 to 0.09375
- k_prev: float32 [12288, 12288], P('row', 'col'), as said below
- energies: float32 [12288], P('row'), may hold values from 0.3 to 2
Outputs:
- casida: float32 [12288, 12288], P('row', 'col')
- vectors: float32 [12288, 8], P('row')
- images: float32 [12288, 8], P('row')
- tridiagonal: float32 [2, 8], replicated
Inputs may be any that keep to these rules, and one draw needn't show every extreme that they name: k_prev is exactly symmetric.
All inputs are finite; a program needn't handle non-finite values.
Results may differ from a plain program's by a relative error of at most 0.0003.
Values sent between devices are 32-bit elements; how exact they have to be, the bound alone decides.
No kernel may reach another device: no remote copies, remote signals or barrier semaphores. Data moves between devices by JAX's collectives and lax.ppermute only.
A program may use at most 128 MiB of HBM per device.

v0:
```python
import jax
import jax.numpy as jnp
from jax import lax
from jax.sharding import PartitionSpec as P

N = 12288
PANEL_W = 512
PC = 8


def from_root(value, axis, root):
    mine = lax.axis_index(axis) == root
    return lax.psum(jnp.where(mine, value, jnp.zeros_like(value)), axis)


def shards(pair_factors, k_prev, energies):
    rows_here, cols_here = k_prev.shape
    per_col = lax.axis_size("row") // lax.axis_size("col")
    row_index = lax.axis_index("row")
    col_index = lax.axis_index("col")
    total = jnp.zeros((rows_here, cols_here), jnp.float32)
    aux_here = pair_factors.shape[1]
    width = PANEL_W
    for start_at in range(0, aux_here, width):
        stop_at = min(start_at + width, aux_here)
        piece = pair_factors[:, start_at:stop_at]
        left_rows = lax.all_gather(piece, "col", axis=0, tiled=True)
        right_parts = []
        for offset in range(per_col):
            right_parts.append(from_root(left_rows, "row", per_col * col_index + offset))
        right_rows = jnp.concatenate(right_parts, axis=0)
        total = total + lax.dot_general(
            left_rows,
            right_rows,
            (((1,), (1,)), ((), ())),
            precision=lax.Precision.HIGHEST,
            preferred_element_type=jnp.float32,
        )
    global_rows = row_index * rows_here + jnp.arange(rows_here, dtype=jnp.int32)
    global_cols = col_index * cols_here + jnp.arange(cols_here, dtype=jnp.int32)
    on_diagonal = global_rows[:, None] == global_cols[None, :]
    casida = 4.0 * (k_prev + total) + jnp.where(on_diagonal, energies[:, None], 0.0)
    col_ids = jnp.arange(PC, dtype=jnp.int32)
    scale = jnp.sqrt(jnp.float32(N))
    diag_list = []
    sub_list = []
    spread = from_root(casida[:, :PC], "col", 0)
    panel = lax.all_gather(spread, "row", axis=0, tiled=True)
    total_rows = panel.shape[0]
    all_rows = jnp.arange(total_rows, dtype=jnp.int32)
    upper_full = jnp.zeros((total_rows, PC), jnp.float32)
    lower_full = jnp.zeros((total_rows, PC), jnp.float32)
    for column_at in range(PC):
        column = (
            panel[:, column_at]
            - jnp.dot(upper_full, lower_full[column_at], precision=lax.Precision.HIGHEST)
            - jnp.dot(lower_full, upper_full[column_at], precision=lax.Precision.HIGHEST)
        )
        diag_list.append(column[column_at])
        below = jnp.where(all_rows > column_at, column, 0.0)
        lead = column[column_at + 1]
        sigma = jnp.sum(below * below)
        root = jnp.sqrt(sigma)
        alpha = jnp.where(lead >= 0, -root, root)
        length = jnp.sqrt(jnp.maximum(2.0 * (sigma + jnp.abs(lead) * root), 1.0))
        unit = (below - alpha * (all_rows == column_at + 1).astype(jnp.float32)) / length
        unit_cols = lax.dynamic_slice_in_dim(unit, col_index * cols_here, cols_here, 0)
        partial_rows = jnp.dot(casida, unit_cols, precision=lax.Precision.HIGHEST)
        placed = lax.dynamic_update_slice_in_dim(
            jnp.zeros((total_rows,), jnp.float32), partial_rows, row_index * rows_here, 0
        )
        image = lax.psum(placed, ("row", "col"))
        image = image - jnp.dot(
            upper_full,
            jnp.dot(lower_full.T, unit, precision=lax.Precision.HIGHEST),
            precision=lax.Precision.HIGHEST,
        )
        image = image - jnp.dot(
            lower_full,
            jnp.dot(upper_full.T, unit, precision=lax.Precision.HIGHEST),
            precision=lax.Precision.HIGHEST,
        )
        image = 2.0 * image
        partner = image - jnp.sum(image * unit) * unit
        pick = (col_ids == column_at).astype(jnp.float32)[None, :]
        upper_full = upper_full + unit[:, None] * pick
        lower_full = lower_full + partner[:, None] * pick
        sub_list.append(alpha)
    upper = lax.dynamic_slice_in_dim(upper_full, row_index * rows_here, rows_here, 0)
    lower = lax.dynamic_slice_in_dim(lower_full, row_index * rows_here, rows_here, 0)
    tridiagonal = jnp.stack([jnp.stack(diag_list), jnp.stack(sub_list)])
    return (casida, scale * upper, scale * lower, tridiagonal)


def solution(mesh):
    in_specs = (P(("row", "col"), None), P("row", "col"), P("row"))
    out_specs = (P("row", "col"), P("row", None), P("row", None), P())
    return jax.shard_map(shards, mesh=mesh, in_specs=in_specs, out_specs=out_specs, check_vma=False)
```

profile of v0, /device:TPU:0, one launch (start us, length us, event | category | flops | bytes accessed | tf_op | source)
XLA Modules:
  0.0 965.6 jit_solution(18281307544850483089)
XLA Ops:
  10.7 65.6 %all-gather.5.cloned.1.call-done = f32[1536,512]{1,0:T(8,128)} async-done(((f32[384,512]{1,0:T(8,128)}), f32[1536,512]{1,0:T(8,128)}) %all-gather.5.cloned.1.call-update) | async-done | bytes 3145744 | tf_op jit(solution)/shard_map/all_gather | solution.py:27
  81.9 58.1 %all-gather.3.cloned.1.call-done = f32[1536,512]{1,0:T(8,128)} async-done(((f32[384,512]{1,0:T(8,128)}), f32[1536,512]{1,0:T(8,128)}) %all-gather.3.cloned.1.call-update) | async-done | bytes 3145744 | tf_op jit(solution)/shard_map/all_gather | solution.py:27
  146.3 18.8 %copy.9 = f32[1536,3072]{0,1:T(8,128)} copy(f32[1536,3072]{1,0:T(8,128)} %param.4) | data formatting | bytes 37748736 | tf_op args[1]
  165.1 151.2 %all-reduce.3.cloned.1.call-done = (f32[1536,512]{1,0:T(8,128)}, f32[1536,512]{1,0:T(8,128)}, f32[1536,512]{1,0:T(8,128)}, f32[1536,512]{1,0:T(8,128)}) async-done(((f32[1536,512]{1,0:T(8,128)}, f32[1536,512]{1,0:T(8,128)}, f32[1536,512]{1,0:T(8,128)}, f32[1536,512]{1,0:T(8,128)}), (f32[1536,512]{1,0:T(8,128)}, f32[1536,512]{1,0:T(8,128)}, f32[1536,512]{1,0:T(8,128)}, ...) | async-done | bytes 12582928 | tf_op jit(solution)/shard_map/psum | solution.py:13
  316.4 34.6 %fusion.2 = f32[3072,1536]{1,0:T(8,128)} fusion(f32[1536,512]{1,0:T(8,128)S(1)} %copy-done.1, f32[1536,512]{1,0:T(8,128)} %get-tuple-element.12, f32[1536,512]{1,0:T(8,128)} %get-tuple-element.13), kind=kOutput, calls=%fused_computation.3 | convolution fusion | flops 28992602112 | bytes 28311552 | tf_op jit(solution)/shard_map/dot_general | solution.py:32
  351.0 39.2 %fusion.1 = f32[1536,3072]{0,1:T(8,128)S(1)} fusion(f32[1536,3072]{0,1:T(8,128)} %copy.9, f32[3072,1536]{1,0:T(8,128)} %fusion.2, f32[1536,512]{1,0:T(8,128)} %all-gather.5.cloned.1.call-done, f32[1536]{0:T(1024)S(1)} %copy-done.2, s32[1536]{0:T(1024)S(1)} %iota_add_fusion.1, s32[3072]{0:T(1024)S(1)} %iota_add_fusion, f32[1536,512]{1,0:T(8,128)} %get-tuple-element.14, ...), kind=kOutput, calls=%fused_computation.2 | convolution fusion | flops 29020913664 | bytes 66084864 | tf_op jit(solution)/shard_map/dot_general | solution.py:32
  396.7 19.5 %psum.95 = f32[1536,8]{0,1:T(8,128)S(1)} all-reduce(f32[1536,8]{0,1:T(8,128)S(1)} %slice_select_fusion), channel_id=1, replica_groups=mesh['row'=8,'col'=4] {'col'}, use_global_device_ids=true, to_apply=%region_4.5 | all-reduce | flops 12288 | bytes 98304 | tf_op jit(solution)/shard_map/psum | solution.py:13
  430.6 12.9 %convolution_reduce_fusion.7 = f32[1536]{0:T(1024)S(1)} fusion(f32[1536,3072]{0,1:T(8,128)} %copy-done, f32[3072,1]{0,1:T(1,128)S(1)} %bitcast.304), kind=kOutput, calls=%fused_computation.21 | convolution fusion | flops 56623104 | bytes 18892800 | tf_op jit(solution)/shard_map/dot_general | solution.py:68
  443.8 38.0 %psum.96 = f32[12288]{0:T(1024)S(1)} all-reduce(f32[12288]{0:T(1024)S(1)} %dynamic_update_slice.24), channel_id=1, replica_groups=mesh['row'=8,'col'=4] {'row','col'}, use_global_device_ids=true, to_apply=%region_6.7 | all-reduce | flops 12288 | bytes 98304 | tf_op jit(solution)/shard_map/psum | solution.py:72
  493.4 12.9 %convolution_reduce_fusion.6 = f32[1536]{0:T(1024)S(1)} fusion(f32[1536,3072]{0,1:T(8,128)} %copy-done, f32[3072,1]{0,1:T(1,128)S(1)} %bitcast.298), kind=kOutput, calls=%fused_computation.20 | convolution fusion | flops 56623104 | bytes 18892800 | tf_op jit(solution)/shard_map/dot_general | solution.py:68
  506.6 41.5 %psum.97 = f32[12288]{0:T(1024)S(1)} all-reduce(f32[12288]{0:T(1024)S(1)} %dynamic_update_slice.25), channel_id=1, replica_groups=mesh['row'=8,'col'=4] {'row','col'}, use_global_device_ids=true, to_apply=%region_9.10 | all-reduce | flops 12288 | bytes 98304 | tf_op jit(solution)/shard_map/psum | solution.py:72
  558.1 12.9 %convolution_reduce_fusion.5 = f32[1536]{0:T(1024)S(1)} fusion(f32[1536,3072]{0,1:T(8,128)} %copy-done, f32[3072,1]{0,1:T(1,128)S(1)} %bitcast.299), kind=kOutput, calls=%fused_computation.19 | convolution fusion | flops 56623104 | bytes 18892800 | tf_op jit(solution)/shard_map/dot_general | solution.py:68
  571.3 39.9 %psum.98 = f32[12288]{0:T(1024)S(1)} all-reduce(f32[12288]{0:T(1024)S(1)} %dynamic_update_slice.26), channel_id=1, replica_groups=mesh['row'=8,'col'=4] {'row','col'}, use_global_device_ids=true, to_apply=%region_12.13 | all-reduce | flops 12288 | bytes 98304 | tf_op jit(solution)/shard_map/psum | solution.py:72
  621.3 12.9 %convolution_reduce_fusion.4 = f32[1536]{0:T(1024)S(1)} fusion(f32[1536,3072]{0,1:T(8,128)} %copy-done, f32[3072,1]{0,1:T(1,128)S(1)} %bitcast.300), kind=kOutput, calls=%fused_computation.18 | convolution fusion | flops 56623104 | bytes 18892800 | tf_op jit(solution)/shard_map/dot_general | solution.py:68
  634.5 41.6 %psum.99 = f32[12288]{0:T(1024)S(1)} all-reduce(f32[12288]{0:T(1024)S(1)} %dynamic_update_slice.27), channel_id=1, replica_groups=mesh['row'=8,'col'=4] {'row','col'}, use_global_device_ids=true, to_apply=%region_15.16 | all-reduce | flops 12288 | bytes 98304 | tf_op jit(solution)/shard_map/psum | solution.py:72
  686.5 12.9 %convolution_reduce_fusion.3 = f32[1536]{0:T(1024)S(1)} fusion(f32[1536,3072]{0,1:T(8,128)} %copy-done, f32[3072,1]{0,1:T(1,128)S(1)} %bitcast.301), kind=kOutput, calls=%fused_computation.17 | convolution fusion | flops 56623104 | bytes 18892800 | tf_op jit(solution)/shard_map/dot_general | solution.py:68
  699.7 40.0 %psum.100 = f32[12288]{0:T(1024)S(1)} all-reduce(f32[12288]{0:T(1024)S(1)} %dynamic_update_slice.28), channel_id=1, replica_groups=mesh['row'=8,'col'=4] {'row','col'}, use_global_device_ids=true, to_apply=%region_18.19 | all-reduce | flops 12288 | bytes 98304 | tf_op jit(solution)/shard_map/psum | solution.py:72
  750.0 12.9 %convolution_reduce_fusion.2 = f32[1536]{0:T(1024)S(1)} fusion(f32[1536,3072]{0,1:T(8,128)} %copy-done, f32[3072,1]{0,1:T(1,128)S(1)} %bitcast.302), kind=kOutput, calls=%fused_computation.16 | convolution fusion | flops 56623104 | bytes 18892800 | tf_op jit(solution)/shard_map/dot_general | solution.py:68
  763.3 41.2 %psum.101 = f32[12288]{0:T(1024)S(1)} all-reduce(f32[12288]{0:T(1024)S(1)} %dynamic_update_slice.29), channel_id=1, replica_groups=mesh['row'=8,'col'=4] {'row','col'}, use_global_device_ids=true, to_apply=%region_21.22 | all-reduce | flops 12288 | bytes 98304 | tf_op jit(solution)/shard_map/psum | solution.py:72
  814.5 12.9 %convolution_reduce_fusion.1 = f32[1536]{0:T(1024)S(1)} fusion(f32[1536,3072]{0,1:T(8,128)} %copy-done, f32[3072,1]{0,1:T(1,128)S(1)} %bitcast.303), kind=kOutput, calls=%fused_computation.15 | convolution fusion | flops 56623104 | bytes 18892800 | tf_op jit(solution)/shard_map/dot_general | solution.py:68
  827.7 40.0 %psum.102 = f32[12288]{0:T(1024)S(1)} all-reduce(f32[12288]{0:T(1024)S(1)} %dynamic_update_slice.30), channel_id=1, replica_groups=mesh['row'=8,'col'=4] {'row','col'}, use_global_device_ids=true, to_apply=%region_24.25 | all-reduce | flops 12288 | bytes 98304 | tf_op jit(solution)/shard_map/psum | solution.py:72
  877.0 18.6 %copy.10 = f32[1536,3072]{1,0:T(8,128)} copy(f32[1536,3072]{0,1:T(8,128)} %copy-done) | data formatting | bytes 37748736
  896.1 12.9 %convolution_reduce_fusion = f32[1536]{0:T(1024)S(1)} fusion(f32[1536,3072]{0,1:T(8,128)} %copy-done, f32[3072,1]{0,1:T(1,128)S(1)} %bitcast.297), kind=kOutput, calls=%fused_computation.14 | convolution fusion | flops 56623104 | bytes 18892800 | tf_op jit(solution)/shard_map/dot_general | solution.py:68
  909.3 41.0 %psum.103 = f32[12288]{0:T(1024)S(1)} all-reduce(f32[12288]{0:T(1024)S(1)} %dynamic_update_slice.31), channel_id=1, replica_groups=mesh['row'=8,'col'=4] {'row','col'}, use_global_device_ids=true, to_apply=%region_27.28 | all-reduce | flops 12288 | bytes 98304 | tf_op jit(solution)/shard_map/psum | solution.py:72
  (164 shorter events, 98.0 us)
Async XLA Ops:
  7.2 69.2 %all-gather.5.cloned.1.call-start = ((), (), s32[]{:S(2)}) async-start(), calls=%async_computation.1 | async-start | bytes 3932160 | tf_op jit(solution)/shard_map/all_gather | solution.py:27
  9.9 130.1 %all-gather.3.cloned.1.call-start = ((), (), s32[]{:S(2)}) async-start(), calls=%async_computation | async-start | bytes 3932160 | tf_op jit(solution)/shard_map/all_gather | solution.py:27
  10.6 305.7 %all-reduce.3.cloned.1.call-start = ((), (), s32[]{:S(2)}) async-start(), calls=%async_computation.2 | async-start | bytes 25165824 | tf_op jit(solution)/shard_map/psum | solution.py:13
  146.3 170.1 %copy-start.1 = (f32[1536,512]{1,0:T(8,128)S(1)}, f32[1536,512]{1,0:T(8,128)}, u32[]{:S(2)}) copy-start(f32[1536,512]{1,0:T(8,128)} %all-gather.3.cloned.1.call-done) | copy-start | bytes 9437188
  165.0 185.9 %copy-start.2 = (f32[1536]{0:T(1024)S(1)}, f32[1536]{0:T(1024)}, u32[]{:S(2)}) copy-start(f32[1536]{0:T(1024)} %param.5) | copy-start | bytes 18436
  390.2 6.5 copy-start
Sparse Core Ops, SparseCore 0:
  10.1 66.1 all-gather.4
  77.9 62.0 all-gather.2
  145.7 170.6 all-reduce.2
where the time goes:
time: 974 us; the launch traced here: 966 us
  blocking collectives  352 us (36%)
  waiting for transfers between devices  276 us (28%)
  matrix products  208 us (21%)
  local copies, waits for them, and re-layouts  63.6 us (7%)
  between operations  35.8 us (4%)
  other arithmetic  30 us (3%)
    psum x8, blocking collectives, shards(): image = lax.psum(placed, ('row', 'col'))  323 us
    psum x1, waiting for transfers between devices, from_root(): return lax.psum(jnp.where(mine, value, jnp.zeros_like(value)), axis)  151 us
    all_gather x2, waiting for transfers between devices, shards(): left_rows = lax.all_gather(piece, 'col', axis=0, tiled=True)  124 us
    dot_general x8, matrix products, shards(): partial_rows = jnp.dot(casida, unit_cols, precision=lax.Precision.HIGHEST)  103 us
    dot_general x2, matrix products, shards(): lax.dot_general(left_rows, right_rows, (((1,), (1,)), ((), ())), precisio...  73.9 us
    unnamed x8, local copies, waits for them, and re-layouts  43.9 us
  transfers between devices with their start and end apart: 3, of which 3 were waited for; matrix products, arithmetic and copies ran while one was open for 3% of the time, Pallas kernels for 0%

commit v1 on v0

--- a/solution.py
+++ b/solution.py
@@ -1,3 +1,4 @@
+import functools
 import jax
 import jax.numpy as jnp
 from jax import lax
@@ -6,6 +7,13 @@
 N = 12288
 PANEL_W = 512
 PC = 8
+
+
+def _state_unit(z, device_axis):
+    return jnp.sum(lax.all_gather(z, device_axis), axis=0)
+
+
+groups_settle = functools.partial(_state_unit, device_axis=("row", "col"))
 
 
 def from_root(value, axis, root):
@@ -69,7 +77,7 @@
         placed = lax.dynamic_update_slice_in_dim(
             jnp.zeros((total_rows,), jnp.float32), partial_rows, row_index * rows_here, 0
         )
-        image = lax.psum(placed, ("row", "col"))
+        image = groups_settle(placed)
         image = image - jnp.dot(
             upper_full,
             jnp.dot(lower_full.T, unit, precision=lax.Precision.HIGHEST),

time: 974 us -> 1060 us (1.088)
  waiting for transfers between devices: 276 us -> 656 us
  blocking collectives: 352 us -> 29 us
  other arithmetic: 30 us -> 49.4 us
    all_gather x0 -> x8, waiting for transfers between devices: none -> 380 us  [_state_unit(): return jnp.sum(lax.all_gather(z, device_axis), axis=0)]
    psum x8 -> x0, blocking collectives: 323 us -> none  [shards(): image = lax.psum(placed, ('row', 'col'))]
    reduce_sum x0 -> x8, other arithmetic: none -> 19.5 us  [_state_unit(): return jnp.sum(lax.all_gather(z, device_axis), axis=0)]
    unnamed x8 -> x32, local copies, waits for them, and re-layouts: 43.9 us -> 49.1 us
  transfers between devices with their start and end apart: 3 -> 11, of which waited for: 3 -> 11; matrix products, arithmetic and copies ran while one was open for 3% -> 7% of each run, Pallas kernels for 0% -> 0%
where the time goes in v1:
time: 1060 us; the launch traced here: 1050 us
  waiting for transfers between devices  656 us (62%)
  matrix products  208 us (20%)
  local copies, waits for them, and re-layouts  65.9 us (6%)
  other arithmetic  49.4 us (5%)
  between operations  36.5 us (3%)
  blocking collectives  29 us (3%)
    all_gather x8, waiting for transfers between devices, _state_unit(): return jnp.sum(lax.all_gather(z, device_axis), axis=0)  380 us
    psum x1, waiting for transfers between devices, from_root(): return lax.psum(jnp.where(mine, value, jnp.zeros_like(value)), axis)  151 us
    all_gather x2, waiting for transfers between devices, shards(): left_rows = lax.all_gather(piece, 'col', axis=0, tiled=True)  124 us
    dot_general x8, matrix products, shards(): partial_rows = jnp.dot(casida, unit_cols, precision=lax.Precision.HIGHEST)  103 us
    dot_general x2, matrix products, shards(): lax.dot_general(left_rows, right_rows, (((1,), (1,)), ((), ())), precisio...  73.9 us
    unnamed x32, local copies, waits for them, and re-layouts  49.1 us
  transfers between devices with their start and end apart: 11, of which 11 were waited for; matrix products, arithmetic and copies ran while one was open for 7% of the time, Pallas kernels for 0%

profile of v1, /device:TPU:0, one launch (start us, length us, event | category | flops | bytes accessed | tf_op | source)
XLA Modules:
  0.0 1047.5 jit_solution(3364528772317648115)
XLA Ops:
  10.7 65.6 %all-gather.21.cloned.1.call-done = f32[1536,512]{1,0:T(8,128)} async-done(((f32[384,512]{1,0:T(8,128)}), f32[1536,512]{1,0:T(8,128)}) %all-gather.21.cloned.1.call-update) | async-done | bytes 3145744 | tf_op jit(solution)/shard_map/all_gather | solution.py:35
  81.9 58.1 %all-gather.19.cloned.1.call-done = f32[1536,512]{1,0:T(8,128)} async-done(((f32[384,512]{1,0:T(8,128)}), f32[1536,512]{1,0:T(8,128)}) %all-gather.19.cloned.1.call-update) | async-done | bytes 3145744 | tf_op jit(solution)/shard_map/all_gather | solution.py:35
  146.3 18.8 %copy.11 = f32[1536,3072]{0,1:T(8,128)} copy(f32[1536,3072]{1,0:T(8,128)} %param.4) | data formatting | bytes 37748736 | tf_op args[1]
  165.1 151.3 %all-reduce.3.cloned.1.call-done = (f32[1536,512]{1,0:T(8,128)}, f32[1536,512]{1,0:T(8,128)}, f32[1536,512]{1,0:T(8,128)}, f32[1536,512]{1,0:T(8,128)}) async-done(((f32[1536,512]{1,0:T(8,128)}, f32[1536,512]{1,0:T(8,128)}, f32[1536,512]{1,0:T(8,128)}, f32[1536,512]{1,0:T(8,128)}), (f32[1536,512]{1,0:T(8,128)}, f32[1536,512]{1,0:T(8,128)}, f32[1536,512]{1,0:T(8,128)}, ...) | async-done | bytes 12582928 | tf_op jit(solution)/shard_map/psum | solution.py:21
  316.4 34.6 %fusion.2 = f32[3072,1536]{1,0:T(8,128)} fusion(f32[1536,512]{1,0:T(8,128)S(1)} %copy-done.1, f32[1536,512]{1,0:T(8,128)} %get-tuple-element.16, f32[1536,512]{1,0:T(8,128)} %get-tuple-element.17), kind=kOutput, calls=%fused_computation.3 | convolution fusion | flops 28992602112 | bytes 28311552 | tf_op jit(solution)/shard_map/dot_general | solution.py:40
  351.0 39.2 %fusion.1 = f32[1536,3072]{0,1:T(8,128)S(1)} fusion(f32[1536,3072]{0,1:T(8,128)} %copy.11, f32[3072,1536]{1,0:T(8,128)} %fusion.2, f32[1536,512]{1,0:T(8,128)} %all-gather.21.cloned.1.call-done, f32[1536]{0:T(1024)S(1)} %copy-done.10, s32[1536]{0:T(1024)S(1)} %iota_add_fusion.1, s32[3072]{0:T(1024)S(1)} %iota_add_fusion, f32[1536,512]{1,0:T(8,128)} %get-tuple-element.18, ...), kind=kOutput, calls=%fused_computation.2 | convolution fusion | flops 29020913664 | bytes 66084864 | tf_op jit(solution)/shard_map/dot_general | solution.py:40
  396.7 19.5 %psum.39 = f32[1536,8]{0,1:T(8,128)S(1)} all-reduce(f32[1536,8]{0,1:T(8,128)S(1)} %slice_select_fusion), channel_id=1, replica_groups=mesh['row'=8,'col'=4] {'col'}, use_global_device_ids=true, to_apply=%region_4.5 | all-reduce | flops 12288 | bytes 98304 | tf_op jit(solution)/shard_map/psum | solution.py:21
  430.6 12.9 %fusion.16 = f32[1,1,12288]{2,1,0:T(1,128)S(1)} fusion(f32[1,1,12288]{2,1,0:T(1,128)S(1)} %broadcast.270.clone, s32[]{:T(128)S(6)} %select_n.118, f32[1536,3072]{0,1:T(8,128)} %copy-done, f32[3072,1]{0,1:T(1,128)S(1)} %bitcast.340), kind=kOutput, calls=%fused_computation.25 | convolution fusion | flops 56623104 | bytes 18892804 | tf_op jit(solution)/shard_map/dot_general | solution.py:76
  446.0 50.5 %all-gather.23.cloned.1.call-done = f32[32,1,12288]{2,1,0:T(1,128)} async-done(((f32[1,1,12288]{2,1,0:T(1,128)}), f32[32,1,12288]{2,1,0:T(1,128)}) %all-gather.23.cloned.1.call-update) | async-done | bytes 1572880 | tf_op jit(solution)/shard_map/all_gather | solution.py:13
  506.3 12.9 %fusion.15 = f32[1,1,12288]{2,1,0:T(1,128)S(1)} fusion(f32[1,1,12288]{2,1,0:T(1,128)S(1)} %broadcast.270.clone.1, s32[]{:T(128)S(6)} %select_n.118, f32[1536,3072]{0,1:T(8,128)} %copy-done, f32[3072,1]{0,1:T(1,128)S(1)} %bitcast.341), kind=kOutput, calls=%fused_computation.23 | convolution fusion | flops 56623104 | bytes 18892804 | tf_op jit(solution)/shard_map/dot_general | solution.py:76
  523.2 50.6 %all-gather.25.cloned.1.call-done = f32[32,1,12288]{2,1,0:T(1,128)} async-done(((f32[1,1,12288]{2,1,0:T(1,128)}), f32[32,1,12288]{2,1,0:T(1,128)}) %all-gather.25.cloned.1.call-update) | async-done | bytes 1572880 | tf_op jit(solution)/shard_map/all_gather | solution.py:13
  583.3 12.9 %fusion.14 = f32[1,1,12288]{2,1,0:T(1,128)S(1)} fusion(f32[1,1,12288]{2,1,0:T(1,128)S(1)} %broadcast.270.clone.2, s32[]{:T(128)S(6)} %select_n.118, f32[1536,3072]{0,1:T(8,128)} %copy-done, f32[3072,1]{0,1:T(1,128)S(1)} %bitcast.342), kind=kOutput, calls=%fused_computation.21 | convolution fusion | flops 56623104 | bytes 18892804 | tf_op jit(solution)/shard_map/dot_general | solution.py:76
  600.3 50.5 %all-gather.27.cloned.1.call-done = f32[32,1,12288]{2,1,0:T(1,128)} async-done(((f32[1,1,12288]{2,1,0:T(1,128)}), f32[32,1,12288]{2,1,0:T(1,128)}) %all-gather.27.cloned.1.call-update) | async-done | bytes 1572880 | tf_op jit(solution)/shard_map/all_gather | solution.py:13
  660.3 12.9 %fusion.13 = f32[1,1,12288]{2,1,0:T(1,128)S(1)} fusion(f32[1,1,12288]{2,1,0:T(1,128)S(1)} %broadcast.270.clone.3, s32[]{:T(128)S(6)} %select_n.118, f32[1536,3072]{0,1:T(8,128)} %copy-done, f32[3072,1]{0,1:T(1,128)S(1)} %bitcast.343), kind=kOutput, calls=%fused_computation.19 | convolution fusion | flops 56623104 | bytes 18892804 | tf_op jit(solution)/shard_map/dot_general | solution.py:76
  677.7 50.3 %all-gather.29.cloned.1.call-done = f32[32,1,12288]{2,1,0:T(1,128)} async-done(((f32[1,1,12288]{2,1,0:T(1,128)}), f32[32,1,12288]{2,1,0:T(1,128)}) %all-gather.29.cloned.1.call-update) | async-done | bytes 1572880 | tf_op jit(solution)/shard_map/all_gather | solution.py:13
  737.5 12.9 %fusion.12 = f32[1,1,12288]{2,1,0:T(1,128)S(1)} fusion(f32[1,1,12288]{2,1,0:T(1,128)S(1)} %broadcast.270.clone.4, s32[]{:T(128)S(6)} %select_n.118, f32[1536,3072]{0,1:T(8,128)} %copy-done, f32[3072,1]{0,1:T(1,128)S(1)} %bitcast.344), kind=kOutput, calls=%fused_computation.17 | convolution fusion | flops 56623104 | bytes 18892804 | tf_op jit(solution)/shard_map/dot_general | solution.py:76
  754.5 50.5 %all-gather.31.cloned.1.call-done = f32[32,1,12288]{2,1,0:T(1,128)} async-done(((f32[1,1,12288]{2,1,0:T(1,128)}), f32[32,1,12288]{2,1,0:T(1,128)}) %all-gather.31.cloned.1.call-update) | async-done | bytes 1572880 | tf_op jit(solution)/shard_map/all_gather | solution.py:13
  814.8 12.9 %fusion.11 = f32[1,1,12288]{2,1,0:T(1,128)S(1)} fusion(f32[1,1,12288]{2,1,0:T(1,128)S(1)} %broadcast.270.clone.5, s32[]{:T(128)S(6)} %select_n.118, f32[1536,3072]{0,1:T(8,128)} %copy-done, f32[3072,1]{0,1:T(1,128)S(1)} %bitcast.345), kind=kOutput, calls=%fused_computation.15 | convolution fusion | flops 56623104 | bytes 18892804 | tf_op jit(solution)/shard_map/dot_general | solution.py:76
  832.0 50.4 %all-gather.33.cloned.1.call-done = f32[32,1,12288]{2,1,0:T(1,128)} async-done(((f32[1,1,12288]{2,1,0:T(1,128)}), f32[32,1,12288]{2,1,0:T(1,128)}) %all-gather.33.cloned.1.call-update) | async-done | bytes 1572880 | tf_op jit(solution)/shard_map/all_gather | solution.py:13
  891.7 12.9 %fusion.10 = f32[1,1,12288]{2,1,0:T(1,128)S(1)} fusion(f32[1,1,12288]{2,1,0:T(1,128)S(1)} %broadcast.270.clone.6, s32[]{:T(128)S(6)} %select_n.118, f32[1536,3072]{0,1:T(8,128)} %copy-done, f32[3072,1]{0,1:T(1,128)S(1)} %bitcast.346), kind=kOutput, calls=%fused_computation.13 | convolution fusion | flops 56623104 | bytes 18892804 | tf_op jit(solution)/shard_map/dot_general | solution.py:76
  908.5 50.8 %all-gather.35.cloned.1.call-done = f32[32,1,12288]{2,1,0:T(1,128)} async-done(((f32[1,1,12288]{2,1,0:T(1,128)}), f32[32,1,12288]{2,1,0:T(1,128)}) %all-gather.35.cloned.1.call-update) | async-done | bytes 1572880 | tf_op jit(solution)/shard_map/all_gather | solution.py:13
  968.4 12.9 %fusion.9 = f32[1,1,12288]{2,1,0:T(1,128)S(1)} fusion(f32[1,1,12288]{2,1,0:T(1,128)S(1)} %broadcast.270, s32[]{:T(128)S(6)} %select_n.118, f32[1536,3072]{0,1:T(8,128)} %copy-done, f32[3072,1]{0,1:T(1,128)S(1)} %bitcast.339), kind=kOutput, calls=%fused_computation.11 | convolution fusion | flops 56623104 | bytes 18892804 | tf_op jit(solution)/shard_map/dot_general | solution.py:76
  981.9 18.7 %copy.12 = f32[1536,3072]{1,0:T(8,128)} copy(f32[1536,3072]{0,1:T(8,128)} %copy-done) | data formatting | bytes 37748736
  1009.3 26.7 %all-gather.37.cloned.1.call-done = f32[32,1,12288]{2,1,0:T(1,128)} async-done(((f32[1,1,12288]{2,1,0:T(1,128)}), f32[32,1,12288]{2,1,0:T(1,128)}) %all-gather.37.cloned.1.call-update) | async-done | bytes 1572880 | tf_op jit(solution)/shard_map/all_gather | solution.py:13
  (196 shorter events, 121.8 us)
Async XLA Ops:
  7.2 69.2 %all-gather.21.cloned.1.call-start = ((), (), s32[]{:S(2)}) async-start(), calls=%async_computation.1 | async-start | bytes 3932160 | tf_op jit(solution)/shard_map/all_gather | solution.py:35
  9.9 130.1 %all-gather.19.cloned.1.call-start = ((), (), s32[]{:S(2)}) async-start(), calls=%async_computation | async-start | bytes 3932160 | tf_op jit(solution)/shard_map/all_gather | solution.py:35
  10.6 305.7 %all-reduce.3.cloned.1.call-start = ((), (), s32[]{:S(2)}) async-start(), calls=%async_computation.10 | async-start | bytes 25165824 | tf_op jit(solution)/shard_map/psum | solution.py:21
  145.6 350.9 %all-gather.23.cloned.1.call-start = ((), (), s32[]{:S(2)}) async-start(), calls=%async_computation.2 | async-start | bytes 1622016 | tf_op jit(solution)/shard_map/all_gather | solution.py:13
  146.3 170.1 %copy-start.1 = (f32[1536,512]{1,0:T(8,128)S(1)}, f32[1536,512]{1,0:T(8,128)}, u32[]{:S(2)}) copy-start(f32[1536,512]{1,0:T(8,128)} %all-gather.19.cloned.1.call-done) | copy-start | bytes 9437188
  316.4 34.6 %copy-start.10 = (f32[1536]{0:T(1024)S(1)}, f32[1536]{0:T(1024)}, u32[]{:S(2)}) copy-start(f32[1536]{0:T(1024)} %param.5) | copy-start | bytes 18436
  390.2 6.5 copy-start
  443.5 0.6 copy-start.2
  444.1 129.7 %all-gather.25.cloned.1.call-start = ((), (), s32[]{:S(2)}) async-start(), calls=%async_computation.3 | async-start | bytes 1622016 | tf_op jit(solution)/shard_map/all_gather | solution.py:13
  519.2 0.6 copy-start.3
  519.8 131.0 %all-gather.27.cloned.1.call-start = ((), (), s32[]{:S(2)}) async-start(), calls=%async_computation.4 | async-start | bytes 1622016 | tf_op jit(solution)/shard_map/all_gather | solution.py:13
  596.2 0.6 copy-start.4
  596.8 131.2 %all-gather.29.cloned.1.call-start = ((), (), s32[]{:S(2)}) async-start(), calls=%async_computation.5 | async-start | bytes 1622016 | tf_op jit(solution)/shard_map/all_gather | solution.py:13
  673.2 0.6 copy-start.5
  673.9 131.2 %all-gather.31.cloned.1.call-start = ((), (), s32[]{:S(2)}) async-start(), calls=%async_computation.6 | async-start | bytes 1622016 | tf_op jit(solution)/shard_map/all_gather | solution.py:13
  750.4 0.6 copy-start.6
  751.0 131.3 %all-gather.33.cloned.1.call-start = ((), (), s32[]{:S(2)}) async-start(), calls=%async_computation.7 | async-start | bytes 1622016 | tf_op jit(solution)/shard_map/all_gather | solution.py:13
  827.7 0.6 copy-start.7
  828.3 131.0 %all-gather.35.cloned.1.call-start = ((), (), s32[]{:S(2)}) async-start(), calls=%async_computation.8 | async-start | bytes 1622016 | tf_op jit(solution)/shard_map/all_gather | solution.py:13
  904.6 0.6 copy-start.8
  905.2 130.8 %all-gather.37.cloned.1.call-start = ((), (), s32[]{:S(2)}) async-start(), calls=%async_computation.9 | async-start | bytes 1622016 | tf_op jit(solution)/shard_map/all_gather | solution.py:13
  981.3 0.6 copy-start.9
Sparse Core Ops, SparseCore 0:
  10.1 66.1 all-gather.20
  77.9 62.0 all-gather.18
  145.7 170.6 all-reduce.2
  444.3 52.2 all-gather.22
  519.9 53.8 all-gather.24
  596.9 53.8 all-gather.26
  674.0 53.9 all-gather.28
  751.1 53.8 all-gather.30
  828.4 53.8 all-gather.32
  905.3 53.8 all-gather.34
  982.0 53.9 all-gather.36
